TPU v7x, 256 devices: a whole 4x4x8 slice. The times are simulated.
256 devices in a mesh: seq: 32 (over x, z_hi, core), grp: 8 (over y, z_lo).
Axes of the slice: x: 4, y: 4, z: 8 (z_hi: 4, z_lo: 2; z = z_hi * 2 + z_lo), core: 2. Of those that a mesh axis runs over, the one named last changes fastest.
Arguments:
- out_grad: bfloat16 [8, 6912, 1024], P('grp', 'seq'), may hold values from -6 to 6
- combine_logits: float32 [8, 6912, 128], P('grp', 'seq'), may hold values from -20 to 330
- expert_out: bfloat16 [8, 128, 1024], P('grp', 'seq'), may hold values from -6 to 6
- slot_in: bfloat16 [8, 128, 1024], P('grp', 'seq'), may hold values from -6 to 6
- router: bfloat16 [128, 1024], P('seq'), may hold values from -0.1875 to 0.1875
- w_gate: bfloat16 [128, 2048, 1024], P('seq', 'grp'), may hold values from -0.1875 to 0.1875
- w_up: bfloat16 [128, 2048, 1024], P('seq', 'grp'), may hold values from -0.1875 to 0.1875
- w_down: bfloat16 [128, 2048, 1024], P('seq', 'grp'), may hold values from -0.125 to 0.125
Outputs:
- token_grad: bfloat16 [8, 6912, 1024], P('grp', 'seq')
- slot_grad: float32 [8, 128, 1024], P('grp', 'seq')
- grad_gate: bfloat16 [128, 2048, 1024], P('seq', 'grp')
- grad_up: bfloat16 [128, 2048, 1024], P('seq', 'grp')
- grad_down: bfloat16 [128, 2048, 1024], P('seq', 'grp')
All inputs are finite; a program needn't handle non-finite values.
Results may differ from a plain program's by a relative error of at most 0.028.
Values may be sent and summed in bfloat16 or wider, within the bound.
A program may use at most 64 MiB of HBM per device.

v0:
```python
import jax
import jax.numpy as jnp
from jax import lax
from jax.sharding import PartitionSpec as P


def sent_to_all(x, axis):
    copies = jnp.broadcast_to(x, (lax.axis_size(axis), *x.shape))
    return lax.all_to_all(copies, axis, split_axis=0, concat_axis=0, tiled=True)


def laid_out(parts, dim):
    parts = jnp.moveaxis(parts, 0, dim)
    dims = parts.shape
    return parts.reshape(*dims[:dim], dims[dim] * dims[dim + 1], *dims[dim + 2 :])


def collect(x, axis, dim):
    parts = sent_to_all(x, axis)
    return laid_out(parts, dim)


def split_up(x, dim, length):
    before, after = (x.shape[:dim], x.shape[dim + 1 :])
    return jnp.moveaxis(x.reshape(*before, length, -1, *after), dim, 0)


def sent_and_summed(x, axis, dim):
    length = lax.axis_size(axis)
    parts = lax.all_to_all(split_up(x, dim, length), axis, 0, 0, tiled=True)
    return jnp.sum(parts.astype(jnp.float32), axis=0)


def slot_backward(inputs, out_grads, w_gate, w_up, w_down):
    gate = jnp.einsum("ged,efd->gef", inputs, w_gate, preferred_element_type=jnp.float32)
    upper = jnp.einsum("ged,efd->gef", inputs, w_up, preferred_element_type=jnp.float32)
    sig = jax.nn.sigmoid(gate)
    hidden = (gate * sig * upper).astype(jnp.bfloat16)
    hidden_grad = jnp.einsum("ged,efd->gef", out_grads, w_down, preferred_element_type=jnp.float32)
    up_grad = (hidden_grad * gate * sig).astype(jnp.bfloat16)
    gate_grad = (hidden_grad * upper * sig * (1.0 + gate * (1.0 - sig))).astype(jnp.bfloat16)
    partial_grad = jnp.einsum("gef,efd->ged", gate_grad, w_gate, preferred_element_type=jnp.float32)
    partial_grad = partial_grad + jnp.einsum(
        "gef,efd->ged", up_grad, w_up, preferred_element_type=jnp.float32
    )
    grad_gate = jnp.einsum(
        "gef,ged->efd", gate_grad, inputs, preferred_element_type=jnp.float32
    ).astype(jnp.bfloat16)
    grad_up = jnp.einsum(
        "gef,ged->efd", up_grad, inputs, preferred_element_type=jnp.float32
    ).astype(jnp.bfloat16)
    grad_down = jnp.einsum(
        "gef,ged->efd", hidden, out_grads, preferred_element_type=jnp.float32
    ).astype(jnp.bfloat16)
    return (partial_grad, grad_gate, grad_up, grad_down)


def per_device(out_grad, combine_logits, expert_out, slot_in, router, w_gate, w_up, w_down):
    grads = out_grad[0]
    probs = jax.nn.softmax(combine_logits[0], axis=-1)
    probs_bf = probs.astype(jnp.bfloat16)
    early_inputs = collect(slot_in, "grp", 0)
    columns = probs_bf
    slot_out = sent_and_summed(
        lax.dot_general(
            columns, grads, (((0,), (0,)), ((), ())), preferred_element_type=jnp.float32
        ).astype(jnp.bfloat16),
        "seq",
        0,
    ).astype(jnp.bfloat16)
    weight_grad = lax.dot_general(
        grads,
        collect(expert_out[0], "seq", 0),
        (((1,), (1,)), ((), ())),
        preferred_element_type=jnp.float32,
    )
    centre = jnp.sum(weight_grad * probs, axis=-1, keepdims=True)
    logit_grad = (probs * (weight_grad - centre)).astype(jnp.bfloat16)
    columns = logit_grad
    token_sum = jnp.dot(columns, collect(router, "seq", 0), preferred_element_type=jnp.float32)
    token_grad = token_sum.astype(jnp.bfloat16)[None]
    all_out = collect(slot_out[None], "grp", 0)
    partial_grad, grad_gate, grad_up, grad_down = slot_backward(
        early_inputs, all_out, w_gate, w_up, w_down
    )
    slot_grad = sent_and_summed(partial_grad.astype(jnp.bfloat16), "grp", 0)
    return (token_grad, slot_grad, grad_gate, grad_up, grad_down)


def solution(mesh):
    return jax.shard_map(
        per_device,
        mesh=mesh,
        in_specs=(
            P("grp", "seq", None),
            P("grp", "seq", None),
            P("grp", "seq", None),
            P("grp", "seq", None),
            P("seq", None),
            P("seq", "grp", None),
            P("seq", "grp", None),
            P("seq", "grp", None),
        ),
        out_specs=(
            P("grp", "seq", None),
            P("grp", "seq", None),
            P("seq", "grp", None),
            P("seq", "grp", None),
            P("seq", "grp", None),
        ),
        check_vma=False,
    )
```

profile of v0, /device:TPU:1, one launch (start us, length us, event | category | flops | bytes accessed | tf_op | source)
XLA Modules:
  0.0 98.3 jit_solution(16445788004871004008)
XLA Ops:
  0.7 1.5 %broadcast_in_dim.23 = bf16[8,1,4,1024]{3,2,1,0:T(4,128)(2,1)} broadcast(bf16[4,1024]{1,0:T(4,128)(2,1)} %bitcast.66), dimensions={2,3} | broadcast | bytes 73728 | tf_op jit(solution)/shard_map/broadcast_in_dim | solution.py:8
  2.2 6.4 %all-to-all-start.4 = ((bf16[8,1,4,1024]{3,2,1,0:T(4,128)(2,1)}), bf16[8,1,4,1024]{3,2,1,0:T(4,128)(2,1)S(1)}, u32[]{:S(2)}, u32[]{:S(2)}) async-start(bf16[8,1,4,1024]{3,2,1,0:T(4,128)(2,1)} %broadcast_in_dim.23), calls=%async_computation.4 | async-start | bytes 131072 | tf_op jit(solution)/shard_map/all_to_all | solution.py:9
  8.5 1.0 %reduce_max.9 = f32[216]{0:T(256)S(1)} reduce(f32[1,216,128]{2,1,0:T(8,128)} %param.9, f32[]{:T(128)} %constant.1.clone.1), dimensions={0,2}, to_apply=%region_0.0 | reduce | flops 27432 | bytes 111460 | tf_op jit(solution)/shard_map/reduce_max | solution.py:60
  9.5 1.1 %fusion.8 = f32[216]{0:T(256)S(1)} fusion(f32[1,216,128]{2,1,0:T(8,128)} %param.9, f32[216]{0:T(256)S(1)} %reduce_max.9), kind=kLoop, calls=%fused_computation.22 | loop fusion | flops 55080 | bytes 112320 | tf_op jit(solution)/shard_map/reduce_sum | solution.py:60
  10.6 1.4 %convolution_convert_fusion.4 = bf16[128,1024]{1,0:T(8,128)(2,1)S(1)} fusion(bf16[1,216,1024]{2,1,0:T(8,128)(2,1)} %param.8, f32[1,216,128]{2,1,0:T(8,128)} %param.9, f32[216]{0:T(256)S(1)} %fusion.8, f32[216]{0:T(256)S(1)} %reduce_max.9), kind=kOutput, calls=%fused_computation.5 | convolution fusion | flops 56837120 | bytes 816832 | tf_op jit(solution)/shard_map/dot_general | solution.py:65
  12.2 1.5 %all-to-all-done.4 = bf16[8,1,4,1024]{3,2,1,0:T(4,128)(2,1)S(1)} async-done(((bf16[8,1,4,1024]{3,2,1,0:T(4,128)(2,1)}), bf16[8,1,4,1024]{3,2,1,0:T(4,128)(2,1)S(1)}, u32[]{:S(2)}, u32[]{:S(2)}) %all-to-all-start.4) | async-done | bytes 65568 | tf_op jit(solution)/shard_map/all_to_all | solution.py:9
  13.7 25.2 %all_to_all.30 = bf16[32,4,1024]{2,1,0:T(4,128)(2,1)S(1)} all-to-all(bf16[32,4,1024]{2,1,0:T(4,128)(2,1)S(1)} %reshape.44), channel_id=1, replica_groups=mesh['seq'=32,'grp'=8] {'seq'}, dimensions={0} | all-to-all | bytes 524288 | tf_op jit(solution)/shard_map/all_to_all | solution.py:30
  38.9 0.8 broadcast_in_dim.19
  39.7 4.2 %all-to-all-start = ((bf16[32,4,1024]{2,1,0:T(4,128)(2,1)}), bf16[32,4,1024]{2,1,0:T(4,128)(2,1)S(1)}, u32[]{:S(2)}, u32[]{:S(2)}) async-start(bf16[32,4,1024]{2,1,0:T(4,128)(2,1)} %broadcast_in_dim.19), calls=%async_computation | async-start | bytes 524288 | tf_op jit(solution)/shard_map/all_to_all | solution.py:9
  44.6 12.3 %all-to-all-done = bf16[32,4,1024]{2,1,0:T(4,128)(2,1)S(1)} async-done(((bf16[32,4,1024]{2,1,0:T(4,128)(2,1)}), bf16[32,4,1024]{2,1,0:T(4,128)(2,1)S(1)}, u32[]{:S(2)}, u32[]{:S(2)}) %all-to-all-start) | async-done | bytes 262176 | tf_op jit(solution)/shard_map/all_to_all | solution.py:9
  56.9 0.8 broadcast_in_dim.20
  57.7 4.5 %all-to-all-start.1 = ((bf16[32,4,1024]{2,1,0:T(4,128)(2,1)}), bf16[32,4,1024]{2,1,0:T(4,128)(2,1)S(1)}, u32[]{:S(2)}, u32[]{:S(2)}) async-start(bf16[32,4,1024]{2,1,0:T(4,128)(2,1)} %broadcast_in_dim.20), calls=%async_computation.1 | async-start | bytes 524288 | tf_op jit(solution)/shard_map/all_to_all | solution.py:9
  62.2 2.9 %convolution_bitcast_fusion.1 = f32[8,4,256]{2,0,1:T(8,128)} fusion(bf16[4,256,1024]{2,1,0:T(8,128)(2,1)} %param.14, bf16[8,1,4,1024]{3,2,1,0:T(4,128)(2,1)S(1)} %all-to-all-done.4), kind=kOutput, calls=%fused_computation.10 | convolution fusion | flops 16777216 | bytes 2195456 | tf_op jit(solution)/shard_map/ged,efd->gef/dot_general | solution.py:36
  65.0 0.8 reshape.42
  65.9 1.3 %multiply_reduce_fusion = (f32[216]{0:T(256)S(1)}, f32[216,128]{1,0:T(8,128)S(1)}) fusion(f32[216]{0:T(256)S(1)} %fusion.8, f32[216]{0:T(256)S(1)} %reduce_max.9, f32[1,216,128]{2,1,0:T(8,128)S(1)} %copy-done.2, bf16[128,1024]{1,0:T(8,128)(2,1)} %reshape.42, bf16[1,216,1024]{2,1,0:T(8,128)(2,1)S(1)} %copy-done.3), kind=kOutput, calls=%fused_computation.20 | convolution fusion | flops 56733480 | bytes 928288 | tf_op jit(solution)/shard_map/dot_general | solution.py:71
  67.3 7.6 %all-to-all-done.1 = bf16[32,4,1024]{2,1,0:T(4,128)(2,1)S(1)} async-done(((bf16[32,4,1024]{2,1,0:T(4,128)(2,1)}), bf16[32,4,1024]{2,1,0:T(4,128)(2,1)S(1)}, u32[]{:S(2)}, u32[]{:S(2)}) %all-to-all-start.1) | async-done | bytes 262176 | tf_op jit(solution)/shard_map/all_to_all | solution.py:9
  75.5 3.4 %all-to-all-start.3 = ((bf16[8,1,4,1024]{3,2,1,0:T(4,128)(2,1)}), bf16[8,1,4,1024]{3,2,1,0:T(4,128)(2,1)S(1)}, u32[]{:S(2)}, u32[]{:S(2)}) async-start(bf16[8,1,4,1024]{3,2,1,0:T(4,128)(2,1)} %broadcast_in_dim.22), calls=%async_computation.3 | async-start | bytes 131072 | tf_op jit(solution)/shard_map/all_to_all | solution.py:9
  78.9 1.1 %fusion = bf16[1,216,1024]{2,1,0:T(8,128)(2,1)} fusion(bf16[128,1024]{1,0:T(8,128)(2,1)S(1)} %reshape.43, f32[216,128]{1,0:T(8,128)S(1)} %get-tuple-element.8, f32[216]{0:T(256)S(1)} %get-tuple-element.7, f32[1,216,128]{2,1,0:T(8,128)S(1)} %copy-done.2, f32[216]{0:T(256)S(1)} %fusion.8, f32[216]{0:T(256)S(1)} %reduce_max.9), kind=kOutput, calls=%fused_computation.4 | convolution fusion | flops 56982528 | bytes 928288 | tf_op jit(solution)/shard_map/dot_general | solution.py:80
  80.1 4.1 %all-to-all-done.3 = bf16[8,1,4,1024]{3,2,1,0:T(4,128)(2,1)S(1)} async-done(((bf16[8,1,4,1024]{3,2,1,0:T(4,128)(2,1)}), bf16[8,1,4,1024]{3,2,1,0:T(4,128)(2,1)S(1)}, u32[]{:S(2)}, u32[]{:S(2)}) %all-to-all-start.3) | async-done | bytes 65568 | tf_op jit(solution)/shard_map/all_to_all | solution.py:9
  84.2 2.4 %multiply_convert_fusion.3 = (bf16[8,4,256]{2,0,1:T(8,128)(2,1)S(1)}, bf16[8,4,256]{2,0,1:T(8,128)(2,1)S(1)}) fusion(f32[8,4,256]{2,0,1:T(8,128)S(1)} %convolution_bitcast_fusion, f32[8,4,256]{2,0,1:T(8,128)S(1)} %copy-done.4, bf16[4,256,1024]{2,1,0:T(8,128)(2,1)} %param.15, bf16[8,1,4,1024]{3,2,1,0:T(4,128)(2,1)S(1)} %all-to-all-done.3), kind=kOutput, calls=%fused_computation.39 | convolution fusion | flops 16883712 | bytes 2260992 | tf_op jit(solution)/shard_map/ged,efd->gef/dot_general | solution.py:39
  88.0 3.3 %all-to-all-start.5 = ((bf16[8,1,4,1024]{3,2,1,0:T(4,128)(2,1)}), bf16[8,1,4,1024]{3,2,1,0:T(4,128)(2,1)S(1)}, u32[]{:S(2)}, u32[]{:S(2)}) async-start(bf16[8,1,4,1024]{3,2,1,0:T(4,128)(2,1)} %copy.15), calls=%async_computation.5 | async-start | bytes 131072 | tf_op jit(solution)/shard_map/all_to_all | solution.py:30
  91.4 2.1 %convolution_convert_fusion = bf16[4,256,1024]{2,1,0:T(8,128)(2,1)} fusion(bf16[8,1,4,1024]{3,2,1,0:T(4,128)(2,1)S(1)} %all-to-all-done.3, f32[8,4,256]{2,0,1:T(8,128)S(1)} %copy-done.4, f32[8,4,256]{2,0,1:T(8,128)S(1)} %convolution_bitcast_fusion), kind=kOutput, calls=%fused_computation | convolution fusion | flops 17874944 | bytes 2228224 | tf_op jit(solution)/shard_map/gef,ged->efd/dot_general | solution.py:52
  93.5 2.1 %convolution_convert_fusion.1 = bf16[4,256,1024]{2,1,0:T(8,128)(2,1)} fusion(bf16[8,4,256]{2,0,1:T(8,128)(2,1)S(1)} %get-tuple-element.5, bf16[8,1,4,1024]{3,2,1,0:T(4,128)(2,1)S(1)} %all-to-all-done.4), kind=kOutput, calls=%fused_computation.1 | convolution fusion | flops 17825792 | bytes 2179072 | tf_op jit(solution)/shard_map/gef,ged->efd/dot_general | solution.py:49
  95.6 2.1 %convolution_convert_fusion.2 = bf16[4,256,1024]{2,1,0:T(8,128)(2,1)} fusion(bf16[8,4,256]{2,0,1:T(8,128)(2,1)S(1)} %get-tuple-element.6, bf16[8,1,4,1024]{3,2,1,0:T(4,128)(2,1)S(1)} %all-to-all-done.4), kind=kOutput, calls=%fused_computation.2 | convolution fusion | flops 17825792 | bytes 2179072 | tf_op jit(solution)/shard_map/gef,ged->efd/dot_general | solution.py:46
  (24 shorter events, 3.7 us)
Async XLA Ops:
  0.6 43.3 %copy-start = (bf16[4,256,1024]{2,1,0:T(8,128)(2,1)S(1)}, bf16[4,256,1024]{2,1,0:T(8,128)(2,1)}, u32[]{:S(2)}) copy-start(bf16[4,256,1024]{2,1,0:T(8,128)(2,1)} %param.13) | copy-start | bytes 6291460
  0.6 38.3 %copy-start.5 = (bf16[1,4,1024]{2,1,0:T(4,128)(2,1)S(1)}, bf16[1,4,1024]{2,1,0:T(4,128)(2,1)}, u32[]{:S(2)}) copy-start(bf16[1,4,1024]{2,1,0:T(4,128)(2,1)} %param.10) | copy-start | bytes 24580
  2.2 11.6 %all-to-all-start.4 = ((bf16[8,1,4,1024]{3,2,1,0:T(4,128)(2,1)}), bf16[8,1,4,1024]{3,2,1,0:T(4,128)(2,1)S(1)}, u32[]{:S(2)}, u32[]{:S(2)}) async-start(bf16[8,1,4,1024]{3,2,1,0:T(4,128)(2,1)} %broadcast_in_dim.23), calls=%async_computation.4 | async-start | bytes 131072 | tf_op jit(solution)/shard_map/all_to_all | solution.py:9
  12.1 44.8 %copy-start.6 = (bf16[4,1024]{1,0:T(4,128)(2,1)S(1)}, bf16[4,1024]{1,0:T(4,128)(2,1)}, u32[]{:S(2)}) copy-start(bf16[4,1024]{1,0:T(4,128)(2,1)} %param.12) | copy-start | bytes 24580
  39.7 17.2 %all-to-all-start = ((bf16[32,4,1024]{2,1,0:T(4,128)(2,1)}), bf16[32,4,1024]{2,1,0:T(4,128)(2,1)S(1)}, u32[]{:S(2)}, u32[]{:S(2)}) async-start(bf16[32,4,1024]{2,1,0:T(4,128)(2,1)} %broadcast_in_dim.19), calls=%async_computation | async-start | bytes 524288 | tf_op jit(solution)/shard_map/all_to_all | solution.py:9
  44.6 21.4 %copy-start.2 = (f32[1,216,128]{2,1,0:T(8,128)S(1)}, f32[1,216,128]{2,1,0:T(8,128)}, u32[]{:S(2)}) copy-start(f32[1,216,128]{2,1,0:T(8,128)} %param.9) | copy-start | bytes 331780
  44.6 21.4 %copy-start.3 = (bf16[1,216,1024]{2,1,0:T(8,128)(2,1)S(1)}, bf16[1,216,1024]{2,1,0:T(8,128)(2,1)}, u32[]{:S(2)}) copy-start(bf16[1,216,1024]{2,1,0:T(8,128)(2,1)} %param.8) | copy-start | bytes 1327108
  57.7 17.2 %all-to-all-start.1 = ((bf16[32,4,1024]{2,1,0:T(4,128)(2,1)}), bf16[32,4,1024]{2,1,0:T(4,128)(2,1)S(1)}, u32[]{:S(2)}, u32[]{:S(2)}) async-start(bf16[32,4,1024]{2,1,0:T(4,128)(2,1)} %broadcast_in_dim.20), calls=%async_computation.1 | async-start | bytes 524288 | tf_op jit(solution)/shard_map/all_to_all | solution.py:9
  65.8 18.4 %copy-start.4 = (f32[8,4,256]{2,0,1:T(8,128)S(1)}, f32[8,4,256]{2,0,1:T(8,128)}, u32[]{:S(2)}) copy-start(f32[8,4,256]{2,0,1:T(8,128)} %convolution_bitcast_fusion.1) | copy-start | bytes 98308
  75.5 8.7 %all-to-all-start.3 = ((bf16[8,1,4,1024]{3,2,1,0:T(4,128)(2,1)}), bf16[8,1,4,1024]{3,2,1,0:T(4,128)(2,1)S(1)}, u32[]{:S(2)}, u32[]{:S(2)}) async-start(bf16[8,1,4,1024]{3,2,1,0:T(4,128)(2,1)} %broadcast_in_dim.22), calls=%async_computation.3 | async-start | bytes 131072 | tf_op jit(solution)/shard_map/all_to_all | solution.py:9
  84.2 2.8 %copy-start.1 = (bf16[4,256,1024]{2,1,0:T(8,128)(2,1)S(1)}, bf16[4,256,1024]{2,1,0:T(8,128)(2,1)}, u32[]{:S(2)}) copy-start(bf16[4,256,1024]{2,1,0:T(8,128)(2,1)} %param.14) | copy-start | bytes 6291460
  88.0 9.6 %all-to-all-start.5 = ((bf16[8,1,4,1024]{3,2,1,0:T(4,128)(2,1)}), bf16[8,1,4,1024]{3,2,1,0:T(4,128)(2,1)S(1)}, u32[]{:S(2)}, u32[]{:S(2)}) async-start(bf16[8,1,4,1024]{3,2,1,0:T(4,128)(2,1)} %copy.15), calls=%async_computation.5 | async-start | bytes 131072 | tf_op jit(solution)/shard_map/all_to_all | solution.py:30
where the time goes:
time: 99.1 us; the launch traced here: 98.3 us
  waiting for transfers between devices  25.6 us (26%)
  blocking collectives  25.2 us (25%)
  starting transfers between devices  21.7 us (22%)
  matrix products  16.8 us (17%)
  local copies, waits for them, and re-layouts  5.35 us (5%)
  other arithmetic  2.86 us (3%)
    all_to_all x4, waiting for transfers between devices, sent_to_all(): return lax.all_to_all(copies, axis, split_axis=0, concat_axis=0, tiled=True)  25.6 us
    all_to_all x1, blocking collectives, sent_and_summed(): parts = lax.all_to_all(split_up(x, dim, length), axis, 0, 0, tiled=True)  25.2 us
    all_to_all x4, starting transfers between devices, sent_to_all(): return lax.all_to_all(copies, axis, split_axis=0, concat_axis=0, tiled=True)  18.4 us
    broadcast_in_dim x4, local copies, waits for them, and re-layouts, sent_to_all(): copies = jnp.broadcast_to(x, (lax.axis_size(axis), *x.shape))  3.69 us
    all_to_all x1, starting transfers between devices, sent_and_summed(): parts = lax.all_to_all(split_up(x, dim, length), axis, 0, 0, tiled=True)  3.35 us
    dot_general x1, matrix products, slot_backward(): jnp.einsum('ged,efd->gef', inputs, w_up, preferred_element_type=jnp.float32)  2.87 us
    dot_general x1, matrix products, slot_backward(): jnp.einsum('ged,efd->gef', out_grads, w_down, preferred_element_type=jnp....  2.4 us
    dot_general x1, matrix products, slot_backward(): jnp.einsum('gef,ged->efd', hidden, out_grads, preferred_element_type=jnp....  2.09 us
  transfers between devices with their start and end apart: 5, of which 4 were waited for; matrix products, arithmetic and copies ran while one was open for 17% of the time, Pallas kernels for 0%

commit v1 on v0

v1 whole, which is shorter than its diff:
```python
import functools

import jax
import jax.numpy as jnp
from jax import lax
from jax.experimental import pallas as pl
from jax.experimental.pallas import tpu as pltpu
from jax.sharding import PartitionSpec as P

MESH = pl.DeviceIdType.MESH
BF = jnp.bfloat16
F32 = jnp.float32
NT = (((1,), (1,)), ((), ()))
TN = (((0,), (0,)), ((), ()))


def exchange_kernel(
    og_h, lg_h, eo_h, si_h, rt_h, wg_h, wu_h, wd_h,
    sg_o, x_o, so_o, gu_o, hi_o, ld_o, rt_o,
    og_v, lg_v, wgu_v, wd_v, er_g, si_g, so_g, sb, xr, ss, rs, ps, pr, probs_v,
    load_sem, d2d_sem, rs_s, rs_r, ag_s, ag_r, zs_s, zs_r, xs_s, xs_r, fw_sem, sx_s, sx_r, pp_s, pp_r,
):
    seq = lax.axis_index("seq")
    grp = lax.axis_index("grp")
    chip = seq // 2
    core = lax.rem(seq, 2)
    x = chip // 4
    zh = lax.rem(chip, 4)
    other = seq + 1 - 2 * core

    loads = [
        pltpu.make_async_copy(lg_h, lg_v, load_sem.at[0]),
        pltpu.make_async_copy(og_h, og_v, load_sem.at[1]),
        pltpu.make_async_copy(si_h, si_g.at[grp], load_sem.at[2]),
        pltpu.make_async_copy(eo_h, er_g.at[0, x, zh, core], load_sem.at[3]),
        pltpu.make_async_copy(rt_h, er_g.at[1, x, zh, core], load_sem.at[4]),
        pltpu.make_async_copy(wg_h, wgu_v.at[pl.ds(0, 1024)], load_sem.at[5]),
        pltpu.make_async_copy(wu_h, wgu_v.at[pl.ds(1024, 1024)], load_sem.at[6]),
        pltpu.make_async_copy(wd_h, wd_v, load_sem.at[7]),
    ]
    for load in loads:
        load.start()

    def chip_at(k):
        return lax.rem(chip + k, 16)

    def group_at(k):
        return lax.rem(grp + k, 8)

    def x_at(k):
        return lax.rem(x + k, 4)

    def z_at(k):
        return lax.rem(zh + k, 4)

    barrier = pltpu.get_barrier_semaphore()

    def greet_chip(k, _):
        pl.semaphore_signal(barrier, inc=1, device_id=(2 * chip_at(k) + core, grp), device_id_type=MESH)
        return 0

    def greet_group(k, _):
        pl.semaphore_signal(barrier, inc=1, device_id=(seq, group_at(k)), device_id_type=MESH)
        return 0

    lax.fori_loop(1, 16, greet_chip, 0)
    lax.fori_loop(1, 8, greet_group, 0)
    pl.semaphore_signal(barrier, inc=1, device_id=(other, grp), device_id_type=MESH)

    loads[0].wait()
    logits = lg_v[...]
    top = jnp.max(logits, axis=-1, keepdims=True)
    raised = jnp.exp(logits - top)
    probs = raised / jnp.sum(raised, axis=-1, keepdims=True)
    probs_v[...] = probs
    loads[1].wait()
    share = lax.dot_general(probs.astype(BF), og_v[...], TN, preferred_element_type=F32)
    sb[...] = share.reshape(16, 2, 4, 1024).astype(BF)

    pl.semaphore_wait(barrier, 23)

    def remote(src, dst, send, recv, device):
        return pltpu.make_async_remote_copy(
            src_ref=src, dst_ref=dst, send_sem=send, recv_sem=recv, device_id=device, device_id_type=MESH
        )

    swap = remote(sb.at[:, 1 - core], xr, d2d_sem.at[0], d2d_sem.at[1], (other, grp))
    swap.start()

    def slot_in_copy(k):
        return remote(si_g.at[grp], si_g.at[grp], sx_s.at[k], sx_r.at[k], (seq, group_at(k)))

    def z_copy(k):
        here = er_g.at[:, x, zh, core]
        return remote(here, here, zs_s.at[k], zs_r.at[k], (2 * (4 * x + z_at(k)) + core, grp))

    def x_copy(k):
        here = er_g.at[:, x, :, core]
        return remote(here, here, xs_s.at[k], xs_r.at[k], (2 * (4 * x_at(k) + zh) + core, grp))

    def share_copy(k):
        return remote(ss.at[chip_at(k)], rs.at[k], rs_s.at[k], rs_r.at[k], (2 * chip_at(k) + core, grp))

    def slot_out_copy(k):
        return remote(so_g.at[grp], so_g.at[grp], ag_s.at[k], ag_r.at[k], (seq, group_at(k)))

    def partial_copy(k):
        return remote(ps.at[group_at(k)], pr.at[k], pp_s.at[k], pp_r.at[k], (seq, group_at(k)))

    def each(first, last, copy, act):
        def step(k, _):
            act(copy(k))
            return 0

        lax.fori_loop(first, last, step, 0)

    def start(c):
        c.start()

    def landed(c):
        c.wait_recv()

    def sent(c):
        c.wait_send()

    loads[2].wait()
    each(1, 8, slot_in_copy, start)
    loads[3].wait()
    loads[4].wait()
    each(1, 4, z_copy, start)

    swap.wait_recv()
    ss[...] = (sb[:, core].astype(F32) + xr[...].astype(F32)).astype(BF)
    each(1, 16, share_copy, start)

    each(1, 8, slot_in_copy, landed)
    inputs = si_g[...].astype(F32).reshape(32, 1024).astype(BF)
    x_o[...] = inputs
    loads[5].wait()
    loads[6].wait()
    gate_up = lax.dot_general(inputs, wgu_v[...], NT, preferred_element_type=F32)
    gate = gate_up[:, :1024]
    upper = gate_up[:, 1024:]
    sig = jax.nn.sigmoid(gate)
    row = lax.broadcasted_iota(jnp.int32, (32, 1024), 0)
    column = lax.broadcasted_iota(jnp.int32, (32, 1024), 1)
    mine = lax.rem(row, 4) == column // 256
    swish = gate * sig
    hi_o[...] = jnp.where(mine, swish * upper, 0.0).astype(BF)
    up_factor = jnp.where(mine, swish, 0.0)
    gate_factor = jnp.where(mine, upper * sig * (1.0 + gate * (1.0 - sig)), 0.0)

    each(1, 4, z_copy, landed)
    each(1, 4, x_copy, start)

    each(1, 16, share_copy, landed)
    total = ss[chip].astype(F32)
    for k in range(1, 16):
        total = total + rs[k].astype(F32)
    so_g[grp] = total.astype(BF)
    each(1, 8, slot_out_copy, start)

    each(1, 4, x_copy, landed)
    gathered = er_g.at[:, :, :, core]
    forward = remote(gathered, gathered, fw_sem.at[0], fw_sem.at[1], (other, grp))
    forward.start()

    loads[7].wait()
    each(1, 8, slot_out_copy, landed)
    slot_outs = so_g[...].astype(F32).reshape(32, 1024).astype(BF)
    so_o[...] = slot_outs
    hidden_grad = lax.dot_general(slot_outs, wd_v[...], NT, preferred_element_type=F32)
    gu = jnp.concatenate([hidden_grad * gate_factor, hidden_grad * up_factor], axis=1).astype(BF)
    gu_o[...] = gu
    partial = jnp.dot(gu, wgu_v[...], preferred_element_type=F32)
    ps[...] = partial.reshape(8, 4, 1024).astype(BF)
    each(1, 8, partial_copy, start)

    forward.wait_recv()
    outs = er_g[0].astype(F32).reshape(128, 1024).astype(BF)
    rt_o[...] = er_g[1].astype(F32).reshape(128, 1024).astype(BF)
    weight_grad = lax.dot_general(og_v[...], outs, NT, preferred_element_type=F32)
    weights = probs_v[...]
    centre = jnp.sum(weight_grad * weights, axis=-1, keepdims=True)
    ld_o[...] = (weights * (weight_grad - centre)).astype(BF)

    each(1, 8, partial_copy, landed)
    total = ps[grp].astype(F32)
    for k in range(1, 8):
        total = total + pr[k].astype(F32)
    sg_o[...] = total

    swap.wait_send()
    each(1, 8, slot_in_copy, sent)
    each(1, 4, z_copy, sent)
    each(1, 4, x_copy, sent)
    each(1, 16, share_copy, sent)
    each(1, 8, slot_out_copy, sent)
    forward.wait_send()
    each(1, 8, partial_copy, sent)


def write_kernel(x_r, so_r, gu_r, hi_r, ld_r, rt_r, tg_h, gg_h, gu_h, gd_h, tg_v, out_v, sem):
    copies = []
    inputs = x_r[...]
    slot_outs = so_r[...]
    for e in range(4):
        rows = pl.ds(256 * e, 256)
        for j, (left, right, dst) in enumerate(
            (
                (gu_r[:, 256 * e : 256 * e + 256], inputs, gg_h),
                (gu_r[:, 1024 + 256 * e : 1280 + 256 * e], inputs, gu_h),
                (hi_r[:, 256 * e : 256 * e + 256], slot_outs, gd_h),
            )
        ):
            out_v[j, rows] = lax.dot_general(left, right, TN, preferred_element_type=F32).astype(BF)
            copy = pltpu.make_async_copy(out_v.at[j, rows], dst.at[rows], sem.at[3 * e + j])
            copy.start()
            copies.append(copy)
    tg_v[...] = jnp.dot(ld_r[...], rt_r[...], preferred_element_type=F32).astype(BF)
    copy = pltpu.make_async_copy(tg_v, tg_h, sem.at[12])
    copy.start()
    copies.append(copy)
    for copy in copies:
        copy.wait()


def per_device(out_grad, combine_logits, expert_out, slot_in, router, w_gate, w_up, w_down):
    any_space = pl.BlockSpec(memory_space=pl.ANY)
    vmem = pl.BlockSpec(memory_space=pltpu.VMEM)
    dma = pltpu.SemaphoreType.DMA
    sds = jax.ShapeDtypeStruct
    slot_grad, x, so, gu, hi, ld, rt = pl.pallas_call(
        exchange_kernel,
        out_shape=(
            sds((4, 1024), F32),
            sds((32, 1024), BF),
            sds((32, 1024), BF),
            sds((32, 2048), BF),
            sds((32, 1024), BF),
            sds((216, 128), BF),
            sds((128, 1024), BF),
        ),
        in_specs=[any_space] * 8,
        out_specs=(vmem,) * 7,
        scratch_shapes=[
            pltpu.VMEM((216, 1024), BF),
            pltpu.VMEM((216, 128), F32),
            pltpu.VMEM((2048, 1024), BF),
            pltpu.VMEM((1024, 1024), BF),
            pltpu.VMEM((2, 4, 4, 2, 4, 1024), BF),
            pltpu.VMEM((8, 4, 1024), BF),
            pltpu.VMEM((8, 4, 1024), BF),
            pltpu.VMEM((16, 2, 4, 1024), BF),
            pltpu.VMEM((16, 4, 1024), BF),
            pltpu.VMEM((16, 4, 1024), BF),
            pltpu.VMEM((16, 4, 1024), BF),
            pltpu.VMEM((8, 4, 1024), BF),
            pltpu.VMEM((8, 4, 1024), BF),
            pltpu.VMEM((216, 128), F32),
            dma((8,)),
            dma((2,)),
            dma((16,)),
            dma((16,)),
            dma((8,)),
            dma((8,)),
            dma((4,)),
            dma((4,)),
            dma((4,)),
            dma((4,)),
            dma((2,)),
            dma((8,)),
            dma((8,)),
            dma((8,)),
            dma((8,)),
        ],
        compiler_params=pltpu.CompilerParams(
            collective_id=0, has_side_effects=True, vmem_limit_bytes=24 * 1024 * 1024
        ),
        name="exchange",
    )(
        out_grad[0],
        combine_logits[0],
        expert_out[0],
        slot_in[0],
        router,
        w_gate.reshape(1024, 1024),
        w_up.reshape(1024, 1024),
        w_down.reshape(1024, 1024),
    )
    token_grad, grad_gate, grad_up, grad_down = pl.pallas_call(
        write_kernel,
        out_shape=(
            sds((216, 1024), BF),
            sds((1024, 1024), BF),
            sds((1024, 1024), BF),
            sds((1024, 1024), BF),
        ),
        in_specs=[vmem] * 6,
        out_specs=(any_space,) * 4,
        scratch_shapes=[
            pltpu.VMEM((216, 1024), BF),
            pltpu.VMEM((3, 1024, 1024), BF),
            dma((13,)),
        ],
        compiler_params=pltpu.CompilerParams(vmem_limit_bytes=24 * 1024 * 1024),
        name="write",
    )(x, so, gu, hi, ld, rt)
    shape = w_gate.shape
    return (
        token_grad[None],
        slot_grad[None],
        grad_gate.reshape(shape),
        grad_up.reshape(shape),
        grad_down.reshape(shape),
    )


def solution(mesh):
    return jax.shard_map(
        per_device,
        mesh=mesh,
        in_specs=(
            P("grp", "seq", None),
            P("grp", "seq", None),
            P("grp", "seq", None),
            P("grp", "seq", None),
            P("seq", None),
            P("seq", "grp", None),
            P("seq", "grp", None),
            P("seq", "grp", None),
        ),
        out_specs=(
            P("grp", "seq", None),
            P("grp", "seq", None),
            P("seq", "grp", None),
            P("seq", "grp", None),
            P("seq", "grp", None),
        ),
        check_vma=False,
    )
```

time: 99.1 us -> 42.5 us (0.43)
  Pallas kernels: 0 us -> 31.8 us
  waiting for transfers between devices: 25.6 us -> 0 us
  blocking collectives: 25.2 us -> 0 us
  starting transfers between devices: 21.7 us -> 0 us
  matrix products: 16.8 us -> 0 us
  local copies, waits for them, and re-layouts: 5.35 us -> 9.37 us
  other arithmetic: 2.86 us -> 0 us
    pallas_call x0 -> x2, Pallas kernels: none -> 31.8 us  [the longest x1 28.5 us: per_device(): pl.pallas_call(exchange_kernel, out_shape=(sds((4, 1024), F32), sds((32,...]
    all_to_all x5 -> x0, waiting for transfers between devices: 25.6 us -> none  [the longest x4 25.6 us: sent_to_all(): return lax.all_to_all(copies, axis, split_axis=0, concat_axis=0, tiled=True)]
    all_to_all x1 -> x0, blocking collectives: 25.2 us -> none  [sent_and_summed(): parts = lax.all_to_all(split_up(x, dim, length), axis, 0, 0, tiled=True)]
    all_to_all x5 -> x0, starting transfers between devices: 21.7 us -> none  [the longest x4 18.4 us: sent_to_all(): return lax.all_to_all(copies, axis, split_axis=0, concat_axis=0, tiled=True)]
    dot_general x11 -> x0, matrix products: 16.8 us -> none  [the longest x1 2.87 us: slot_backward(): jnp.einsum('ged,efd->gef', inputs, w_up, preferred_element_type=jnp.float32)]
    unnamed x14 -> x17, local copies, waits for them, and re-layouts: 0.03 us -> 9.37 us
    broadcast_in_dim x4 -> x0, local copies, waits for them, and re-layouts: 3.69 us -> none  [sent_to_all(): copies = jnp.broadcast_to(x, (lax.axis_size(axis), *x.shape))]
    reduce_sum x3 -> x0, other arithmetic: 1.86 us -> none  [the longest x1 1.08 us: per_device(): probs = jax.nn.softmax(combine_logits[0], axis=-1)]
  transfers between devices with their start and end apart: 5 -> 0, of which waited for: 4 -> 0; matrix products, arithmetic and copies ran while one was open for 17% -> 0% of each run, Pallas kernels for 0% -> 0%
where the time goes in v1:
time: 42.5 us; the launch traced here: 41.8 us
  Pallas kernels  31.8 us (75%)
  local copies, waits for them, and re-layouts  9.37 us (22%)
  between operations  0.67 us (2%)
    pallas_call x1, Pallas kernels, per_device(): pl.pallas_call(exchange_kernel, out_shape=(sds((4, 1024), F32), sds((32,...  28.5 us
    unnamed x17, local copies, waits for them, and re-layouts  9.37 us
    pallas_call x1, Pallas kernels, per_device(): pl.pallas_call(write_kernel, out_shape=(sds((216, 1024), BF), sds((1024,...  3.21 us

profile of v1, /device:TPU:1, one launch (start us, length us, event | category | flops | bytes accessed | tf_op | source)
XLA Modules:
  0.0 41.8 jit_solution(16988858385490647980)
XLA Ops:
  0.6 0.0 copy-start
  0.6 1.6 %copy-done = bf16[4,256,1024]{2,1,0:T(8,128)(2,1)S(1)} copy-done((bf16[4,256,1024]{2,1,0:T(8,128)(2,1)S(1)}, bf16[4,256,1024]{2,1,0:T(8,128)(2,1)}, u32[]{:S(2)}) %copy-start) | copy-done | bytes 2097176
  2.2 0.0 copy-start.1
  2.2 1.6 %copy-done.1 = bf16[4,256,1024]{2,1,0:T(8,128)(2,1)S(1)} copy-done((bf16[4,256,1024]{2,1,0:T(8,128)(2,1)S(1)}, bf16[4,256,1024]{2,1,0:T(8,128)(2,1)}, u32[]{:S(2)}) %copy-start.1) | copy-done | bytes 2097176
  3.8 0.0 copy-start.2
  3.8 1.6 %copy-done.2 = bf16[4,256,1024]{2,1,0:T(8,128)(2,1)S(1)} copy-done((bf16[4,256,1024]{2,1,0:T(8,128)(2,1)S(1)}, bf16[4,256,1024]{2,1,0:T(8,128)(2,1)}, u32[]{:S(2)}) %copy-start.2) | copy-done | bytes 2097176
  5.4 0.0 copy-start.3
  5.4 1.0 %copy-done.3 = bf16[1,216,1024]{2,1,0:T(8,128)(2,1)S(1)} copy-done((bf16[1,216,1024]{2,1,0:T(8,128)(2,1)S(1)}, bf16[1,216,1024]{2,1,0:T(8,128)(2,1)}, u32[]{:S(2)}) %copy-start.3) | copy-done | bytes 442392
  6.4 0.0 copy-start.4
  6.4 0.9 %copy-done.4 = f32[1,216,128]{2,1,0:T(8,128)S(1)} copy-done((f32[1,216,128]{2,1,0:T(8,128)S(1)}, f32[1,216,128]{2,1,0:T(8,128)}, u32[]{:S(2)}) %copy-start.4) | copy-done | bytes 110616
  7.3 0.0 copy-start.5
  7.3 0.7 %copy-done.5 = bf16[1,4,1024]{2,1,0:T(4,128)(2,1)S(1)} copy-done((bf16[1,4,1024]{2,1,0:T(4,128)(2,1)S(1)}, bf16[1,4,1024]{2,1,0:T(4,128)(2,1)}, u32[]{:S(2)}) %copy-start.5) | copy-done | bytes 8216
  8.0 0.0 copy-start.6
  8.0 0.7 %copy-done.6 = bf16[1,4,1024]{2,1,0:T(4,128)(2,1)S(1)} copy-done((bf16[1,4,1024]{2,1,0:T(4,128)(2,1)S(1)}, bf16[1,4,1024]{2,1,0:T(4,128)(2,1)}, u32[]{:S(2)}) %copy-start.6) | copy-done | bytes 8216
  8.7 0.0 copy-start.7
  8.7 0.7 %copy-done.7 = bf16[4,1024]{1,0:T(4,128)(2,1)S(1)} copy-done((bf16[4,1024]{1,0:T(4,128)(2,1)S(1)}, bf16[4,1024]{1,0:T(4,128)(2,1)}, u32[]{:S(2)}) %copy-start.7) | copy-done | bytes 8216
  9.4 28.5 %exchange.1 = (f32[4,1024]{1,0:T(4,128)S(1)}, bf16[32,1024]{1,0:T(8,128)(2,1)S(1)}, bf16[32,1024]{1,0:T(8,128)(2,1)S(1)}, bf16[32,2048]{1,0:T(8,128)(2,1)S(1)}, ...) custom-call(bf16[216,1024]{1,0:T(8,128)(2,1)S(1)} %bitcast.15, ...), custom_call_target="tpu_custom_call" | custom-call | tf_op jit(solution)/shard_map/exchange/pallas_call | solution.py:233
  38.0 3.2 %write.1 = (bf16[216,1024]{1,0:T(8,128)(2,1)}, bf16[1024,1024]{1,0:T(8,128)(2,1)}, bf16[1024,1024]{1,0:T(8,128)(2,1)}, bf16[1024,1024]{1,0:T(8,128)(2,1)}) custom-call(bf16[32,1024]{1,0:T(8,128)(2,1)S(1)} %get-tuple-element.16.x_r, bf16[32,1024]{1,0:T(8,128)(2,1)S(1)} %get-tuple-element.17.so_r, bf16[32,2048]{1,0:T(8,128)(2,1)S(1)} %get-tuple-element.18.gu_r, ...), custom_call_target="tpu_custom_call" | custom-call | tf_op jit(solution)/shard_map/write/pallas_call | solution.py:291
  41.2 0.6 %copy.14 = f32[1,4,1024]{2,1,0:T(4,128)} copy(f32[1,4,1024]{2,1,0:T(4,128)S(1)} %bitcast.17) | data formatting | bytes 32768
Async XLA Ops:
  0.6 1.6 %copy-start = (bf16[4,256,1024]{2,1,0:T(8,128)(2,1)S(1)}, bf16[4,256,1024]{2,1,0:T(8,128)(2,1)}, u32[]{:S(2)}) copy-start(bf16[4,256,1024]{2,1,0:T(8,128)(2,1)} %param.13) | copy-start | bytes 6291460
  2.2 1.6 %copy-start.1 = (bf16[4,256,1024]{2,1,0:T(8,128)(2,1)S(1)}, bf16[4,256,1024]{2,1,0:T(8,128)(2,1)}, u32[]{:S(2)}) copy-start(bf16[4,256,1024]{2,1,0:T(8,128)(2,1)} %param.14) | copy-start | bytes 6291460
  3.8 1.6 %copy-start.2 = (bf16[4,256,1024]{2,1,0:T(8,128)(2,1)S(1)}, bf16[4,256,1024]{2,1,0:T(8,128)(2,1)}, u32[]{:S(2)}) copy-start(bf16[4,256,1024]{2,1,0:T(8,128)(2,1)} %param.15) | copy-start | bytes 6291460
  5.4 1.0 %copy-start.3 = (bf16[1,216,1024]{2,1,0:T(8,128)(2,1)S(1)}, bf16[1,216,1024]{2,1,0:T(8,128)(2,1)}, u32[]{:S(2)}) copy-start(bf16[1,216,1024]{2,1,0:T(8,128)(2,1)} %param.8) | copy-start | bytes 1327108
  6.4 0.9 %copy-start.4 = (f32[1,216,128]{2,1,0:T(8,128)S(1)}, f32[1,216,128]{2,1,0:T(8,128)}, u32[]{:S(2)}) copy-start(f32[1,216,128]{2,1,0:T(8,128)} %param.9) | copy-start | bytes 331780
  7.3 0.7 %copy-start.5 = (bf16[1,4,1024]{2,1,0:T(4,128)(2,1)S(1)}, bf16[1,4,1024]{2,1,0:T(4,128)(2,1)}, u32[]{:S(2)}) copy-start(bf16[1,4,1024]{2,1,0:T(4,128)(2,1)} %param.10) | copy-start | bytes 24580
  8.0 0.7 %copy-start.6 = (bf16[1,4,1024]{2,1,0:T(4,128)(2,1)S(1)}, bf16[1,4,1024]{2,1,0:T(4,128)(2,1)}, u32[]{:S(2)}) copy-start(bf16[1,4,1024]{2,1,0:T(4,128)(2,1)} %param.11) | copy-start | bytes 24580
  8.7 0.7 %copy-start.7 = (bf16[4,1024]{1,0:T(4,128)(2,1)S(1)}, bf16[4,1024]{1,0:T(4,128)(2,1)}, u32[]{:S(2)}) copy-start(bf16[4,1024]{1,0:T(4,128)(2,1)} %rt_h.1) | copy-start | bytes 24580

commit v2 on v1

v2 whole, which is shorter than its diff:
```python
import functools

import jax
import jax.numpy as jnp
from jax import lax
from jax.experimental import pallas as pl
from jax.experimental.pallas import tpu as pltpu
from jax.sharding import PartitionSpec as P

MESH = pl.DeviceIdType.MESH
BF = jnp.bfloat16
F32 = jnp.float32
NT = (((1,), (1,)), ((), ()))
TN = (((0,), (0,)), ((), ()))


def exchange_kernel(
    og_h, lg_h, eo_h, si_h, rt_h, wg_h, wu_h, wd_h,
    gg_o, gu_o, gd_o, tg_o, sg_o,
    og_v, lg_v, wgu_v, wd_v, er_g, si_g, so_g, sb, xr, ss, xb, zp, zb, ps, pr, probs_v, gu_v, hi_v,
    load_sem, swap_sem, rx_s, rx_r, rz_s, rz_r, ag_s, ag_r, zs_s, zs_r, xs_s, xs_r, fw_sem, sx_s, sx_r, pp_s, pp_r,
):
    seq = lax.axis_index("seq")
    grp = lax.axis_index("grp")
    chip = seq // 2
    core = lax.rem(seq, 2)
    x = chip // 4
    zh = lax.rem(chip, 4)
    other = seq + 1 - 2 * core

    loads = [
        pltpu.make_async_copy(lg_h, lg_v, load_sem.at[0]),
        pltpu.make_async_copy(og_h, og_v, load_sem.at[1]),
        pltpu.make_async_copy(si_h, si_g.at[grp], load_sem.at[2]),
        pltpu.make_async_copy(eo_h, er_g.at[0, x, zh, core], load_sem.at[3]),
        pltpu.make_async_copy(rt_h, er_g.at[1, x, zh, core], load_sem.at[4]),
        pltpu.make_async_copy(wg_h, wgu_v.at[pl.ds(0, 1024)], load_sem.at[5]),
        pltpu.make_async_copy(wu_h, wgu_v.at[pl.ds(1024, 1024)], load_sem.at[6]),
        pltpu.make_async_copy(wd_h, wd_v, load_sem.at[7]),
    ]
    for load in loads:
        load.start()

    def group_at(k):
        return lax.rem(grp + k, 8)

    def x_at(k):
        return lax.rem(x + k, 4)

    def z_at(k):
        return lax.rem(zh + k, 4)

    def on_x(k):
        return (2 * (4 * x_at(k) + zh) + core, grp)

    def on_z(k):
        return (2 * (4 * x + z_at(k)) + core, grp)

    def in_group(k):
        return (seq, group_at(k))

    barrier = pltpu.get_barrier_semaphore()

    def greet(device):
        pl.semaphore_signal(barrier, inc=1, device_id=device, device_id_type=MESH)

    for k in (2, 1, 3):
        greet(on_z(k))
    for k in (2, 1, 3):
        greet(on_x(k))
    for k in range(1, 8):
        greet(in_group(k))
    greet((other, grp))

    loads[0].wait()
    logits = lg_v[...]
    top = jnp.max(logits, axis=-1, keepdims=True)
    raised = jnp.exp(logits - top)
    probs = raised / jnp.sum(raised, axis=-1, keepdims=True)
    probs_v[...] = probs
    loads[1].wait()
    share = lax.dot_general(probs.astype(BF), og_v[...], TN, preferred_element_type=F32)
    sb[...] = share.reshape(4, 4, 2, 4, 1024).astype(BF)

    pl.semaphore_wait(barrier, 14)

    def remote(src, dst, send, recv, device):
        return pltpu.make_async_remote_copy(
            src_ref=src, dst_ref=dst, send_sem=send, recv_sem=recv, device_id=device, device_id_type=MESH
        )

    swap = remote(sb.at[:, :, 1 - core], xr, swap_sem.at[0], swap_sem.at[1], (other, grp))
    swap.start()

    slot_in_copies = [
        remote(si_g.at[grp], si_g.at[grp], sx_s.at[k], sx_r.at[k], in_group(k)) for k in range(1, 8)
    ]
    one = er_g.at[:, x, zh, core]
    z_copies = [remote(one, one, zs_s.at[k], zs_r.at[k], on_z(k)) for k in (2, 1, 3)]
    line = er_g.at[:, x, :, core]
    x_copies = [remote(line, line, xs_s.at[k], xs_r.at[k], on_x(k)) for k in (2, 1, 3)]
    plane = er_g.at[:, :, :, core]
    forward = remote(plane, plane, fw_sem.at[0], fw_sem.at[1], (other, grp))
    along_x = {
        k: [
            remote(ss.at[x_at(j), z_at(k)], xb.at[k, j], rx_s.at[k, j], rx_r.at[k, j], on_x(j)) for j in (2, 1, 3)
        ]
        for k in (2, 1, 3, 0)
    }
    along_z = {k: remote(zp.at[k], zb.at[k], rz_s.at[k], rz_r.at[k], on_z(k)) for k in (2, 1, 3)}
    slot_out_copies = [
        remote(so_g.at[grp], so_g.at[grp], ag_s.at[k], ag_r.at[k], in_group(k)) for k in range(1, 8)
    ]
    partial_copies = [
        remote(ps.at[group_at(k)], pr.at[k], pp_s.at[k], pp_r.at[k], in_group(k)) for k in range(1, 8)
    ]

    def start(copies):
        for copy in copies:
            copy.start()

    def landed(copies):
        for copy in copies:
            copy.wait_recv()

    loads[2].wait()
    start(slot_in_copies)
    loads[3].wait()
    loads[4].wait()
    start(z_copies)

    swap.wait_recv()
    ss[...] = (sb[:, :, core].astype(F32) + xr[...].astype(F32)).astype(BF)
    for k in (2, 1, 3, 0):
        start(along_x[k])

    landed(slot_in_copies)
    inputs = si_g[...].astype(F32).reshape(32, 1024).astype(BF)

    for k in (2, 1, 3, 0):
        landed(along_x[k])
        total = ss[x, z_at(k)].astype(F32)
        for j in (1, 2, 3):
            total = total + xb[k, j].astype(F32)
        if k:
            zp[k] = total.astype(BF)
            along_z[k].start()

    landed(z_copies)
    start(x_copies)

    loads[5].wait()
    loads[6].wait()
    gate_up = lax.dot_general(inputs, wgu_v[...], NT, preferred_element_type=F32)
    gate = gate_up[:, :1024]
    upper = gate_up[:, 1024:]
    sig = jax.nn.sigmoid(gate)
    row = lax.broadcasted_iota(jnp.int32, (32, 1024), 0)
    column = lax.broadcasted_iota(jnp.int32, (32, 1024), 1)
    mine = lax.rem(row, 4) == column // 256
    swish = gate * sig
    hi_v[...] = jnp.where(mine, swish * upper, 0.0).astype(BF)
    up_factor = jnp.where(mine, swish, 0.0)
    gate_factor = jnp.where(mine, upper * sig * (1.0 + gate * (1.0 - sig)), 0.0)

    for k in (1, 3, 2):
        along_z[k].wait_recv()
        total = total + zb[k].astype(F32)
    so_g[grp] = total.astype(BF)
    start(slot_out_copies)

    loads[7].wait()
    landed(slot_out_copies)
    slot_outs = so_g[...].astype(F32).reshape(32, 1024).astype(BF)
    hidden_grad = lax.dot_general(slot_outs, wd_v[...], NT, preferred_element_type=F32)
    gu_v[...] = jnp.concatenate([hidden_grad * gate_factor, hidden_grad * up_factor], axis=1).astype(BF)
    partial = jnp.dot(gu_v[...], wgu_v[...], preferred_element_type=F32)
    ps[...] = partial.reshape(8, 4, 1024).astype(BF)
    start(partial_copies)

    landed(x_copies)
    forward.start()

    def outer(left, right, dst, first):
        for e in range(4):
            columns = pl.ds(first + 256 * e, 256)
            dst[pl.ds(256 * e, 256)] = lax.dot_general(
                left[:, columns], right, TN, preferred_element_type=F32
            ).astype(BF)

    outer(gu_v, inputs, gg_o, 0)
    outer(gu_v, inputs, gu_o, 1024)
    outer(hi_v, slot_outs, gd_o, 0)

    forward.wait_recv()
    outs = er_g[0].astype(F32).reshape(128, 1024).astype(BF)
    routes = er_g[1].astype(F32).reshape(128, 1024).astype(BF)
    weight_grad = lax.dot_general(og_v[...], outs, NT, preferred_element_type=F32)
    weights = probs_v[...]
    centre = jnp.sum(weight_grad * weights, axis=-1, keepdims=True)
    logit_grad = (weights * (weight_grad - centre)).astype(BF)
    tg_o[...] = jnp.dot(logit_grad, routes, preferred_element_type=F32).astype(BF)

    landed(partial_copies)
    total = ps[grp].astype(F32)
    for k in range(1, 8):
        total = total + pr[k].astype(F32)
    sg_o[...] = total

    sends = [swap, forward, *slot_in_copies, *z_copies, *x_copies, *along_z.values(), *slot_out_copies]
    for copy in sends + partial_copies + [copy for k in (2, 1, 3, 0) for copy in along_x[k]]:
        copy.wait_send()


def write_kernel(*refs):
    sources, outs, sem = refs[:5], refs[5:10], refs[10]
    copies = [pltpu.make_async_copy(sources[i], outs[i], sem.at[i]) for i in range(5)]
    for copy in copies:
        copy.start()
    for copy in copies:
        copy.wait()


def per_device(out_grad, combine_logits, expert_out, slot_in, router, w_gate, w_up, w_down):
    any_space = pl.BlockSpec(memory_space=pl.ANY)
    vmem = pl.BlockSpec(memory_space=pltpu.VMEM)
    dma = pltpu.SemaphoreType.DMA
    outs = [
        ((1024, 1024), BF),
        ((1024, 1024), BF),
        ((1024, 1024), BF),
        ((216, 1024), BF),
        ((4, 1024), F32),
    ]
    arguments = [
        out_grad[0],
        combine_logits[0],
        expert_out[0],
        slot_in[0],
        router,
        w_gate.reshape(1024, 1024),
        w_up.reshape(1024, 1024),
        w_down.reshape(1024, 1024),
    ]
    block = (4, 1024)
    results = pl.pallas_call(
        exchange_kernel,
        out_shape=[pltpu.VMEM(shape, kind) for shape, kind in outs],
        in_specs=[any_space] * 8,
        out_specs=[vmem] * 5,
        scratch_shapes=[
            pltpu.VMEM((216, 1024), BF),
            pltpu.VMEM((216, 128), F32),
            pltpu.VMEM((2048, 1024), BF),
            pltpu.VMEM((1024, 1024), BF),
            pltpu.VMEM((2, 4, 4, 2, *block), BF),
            pltpu.VMEM((8, *block), BF),
            pltpu.VMEM((8, *block), BF),
            pltpu.VMEM((4, 4, 2, *block), BF),
            pltpu.VMEM((4, 4, *block), BF),
            pltpu.VMEM((4, 4, *block), BF),
            pltpu.VMEM((4, 4, *block), BF),
            pltpu.VMEM((4, *block), BF),
            pltpu.VMEM((4, *block), BF),
            pltpu.VMEM((8, *block), BF),
            pltpu.VMEM((8, *block), BF),
            pltpu.VMEM((216, 128), F32),
            pltpu.VMEM((32, 2048), BF),
            pltpu.VMEM((32, 1024), BF),
            dma((8,)),
            dma((2,)),
            dma((4, 4)),
            dma((4, 4)),
            dma((4,)),
            dma((4,)),
            dma((8,)),
            dma((8,)),
            dma((4,)),
            dma((4,)),
            dma((4,)),
            dma((4,)),
            dma((2,)),
            dma((8,)),
            dma((8,)),
            dma((8,)),
            dma((8,)),
        ],
        compiler_params=pltpu.CompilerParams(
            collective_id=0, has_side_effects=True, vmem_limit_bytes=16 * 1024 * 1024
        ),
        name="exchange",
    )(*[pltpu.with_memory_space_constraint(argument, pltpu.HBM) for argument in arguments])
    grad_gate, grad_up, grad_down, token_grad, slot_grad = pl.pallas_call(
        write_kernel,
        out_shape=[jax.ShapeDtypeStruct(shape, kind) for shape, kind in outs],
        in_specs=[vmem] * 5,
        out_specs=[any_space] * 5,
        scratch_shapes=[dma((5,))],
        compiler_params=pltpu.CompilerParams(vmem_limit_bytes=1024 * 1024),
        name="write",
    )(*results)
    shape = w_gate.shape
    return (
        token_grad[None],
        slot_grad[None],
        grad_gate.reshape(shape),
        grad_up.reshape(shape),
        grad_down.reshape(shape),
    )


def solution(mesh):
    return jax.shard_map(
        per_device,
        mesh=mesh,
        in_specs=(
            P("grp", "seq", None),
            P("grp", "seq", None),
            P("grp", "seq", None),
            P("grp", "seq", None),
            P("seq", None),
            P("seq", "grp", None),
            P("seq", "grp", None),
            P("seq", "grp", None),
        ),
        out_specs=(
            P("grp", "seq", None),
            P("grp", "seq", None),
            P("seq", "grp", None),
            P("seq", "grp", None),
            P("seq", "grp", None),
        ),
        check_vma=False,
    )
```

time: 42.5 us -> 31.2 us (0.73); the launches traced: 41.8 us -> 31.1 us
  local copies, waits for them, and re-layouts: 9.37 us -> 0 us
  Pallas kernels: 31.8 us -> 30.4 us
    unnamed x17 -> x0, local copies, waits for them, and re-layouts: 9.37 us -> none
    pallas_call x2, Pallas kernels: 31.8 us -> 30.4 us  [the longest x1 27.6 us: per_device(): pl.pallas_call(exchange_kernel, out_shape=[pltpu.VMEM(shape, kind) for sh...]
where the time goes in v2:
time: 31.2 us; the launch traced here: 31.1 us
  Pallas kernels  30.4 us (97%)
  between operations  0.64 us (2%)
    pallas_call x1, Pallas kernels, per_device(): pl.pallas_call(exchange_kernel, out_shape=[pltpu.VMEM(shape, kind) for sh...  27.6 us
    pallas_call x1, Pallas kernels, per_device(): pl.pallas_call(write_kernel, out_shape=[jax.ShapeDtypeStruct(shape, kind)...  2.82 us

profile of v2, /device:TPU:1, one launch (start us, length us, event | category | flops | bytes accessed | tf_op | source)
XLA Modules:
  0.0 31.1 jit_solution(82441342234091836)
XLA Ops:
  0.6 27.6 %exchange.1 = (bf16[1024,1024]{1,0:T(8,128)(2,1)S(1)}, bf16[1024,1024]{1,0:T(8,128)(2,1)S(1)}, bf16[1024,1024]{1,0:T(8,128)(2,1)S(1)}, bf16[216,1024]{1,0:T(8,128)(2,1)S(1)}, f32[4,1024]{1,0:T(4,128)S(1)}) custom-call(bf16[216,1024]{1,0:T(8,128)(2,1)} %bitcast.15, f32[216,128]{1,0:T(8,128)} %bitcast.16, bf16[4,1024]{1,0:T(4,128)(2,1)} %bitcast.17, ...), custom_call_target="tpu_custom_call" | custom-call | tf_op jit(solution)/shard_map/exchange/pallas_call | solution.py:246
  28.2 2.8 %write.1 = (bf16[1024,1024]{1,0:T(8,128)(2,1)}, bf16[1024,1024]{1,0:T(8,128)(2,1)}, bf16[1024,1024]{1,0:T(8,128)(2,1)}, bf16[216,1024]{1,0:T(8,128)(2,1)}, f32[4,1024]{1,0:T(4,128)}) custom-call(bf16[1024,1024]{1,0:T(8,128)(2,1)S(1)} %get-tuple-element.15.refs_0_, bf16[1024,1024]{1,0:T(8,128)(2,1)S(1)} %get-tuple-element.16.refs_1_, ...), custom_call_target="tpu_custom_call" | custom-call | tf_op jit(solution)/shard_map/write/pallas_call | solution.py:293
